TPU v7x, 32 devices: a whole 2x2x4 slice. The times are simulated.
32 devices in a mesh: batch: 8 (over z, y), mp: 4 (over x, core).
Axes of the slice: x: 2, y: 2, z: 4, core: 2. Of those that a mesh axis runs over, the one named last changes fastest.
Arguments:
- lookup_ids: int32 [64, 16384], P('batch'), may hold values from 0 to 8191
- table_feature: int32 [64], replicated, may hold values from 0 to 63, each once
- tables: bfloat16 [64, 8192, 128], P('batch'), may hold values from -6 to 6
- cross_down: bfloat16 [2, 8192, 512], P(None, 'mp'), may hold values from -0.0625 to 0.0625
- cross_up: bfloat16 [2, 512, 8192], P(None, None, 'mp'), may hold values from -0.25 to 0.25
- cross_bias: float32 [2, 8192], P(None, 'mp'), may hold values from -3 to 3
Outputs:
- crossed: bfloat16 [16384, 8192], P('batch', 'mp')
Inputs may be any that keep to these rules, and one draw needn't show every extreme that they name: `table_feature`: each number appears once.
All inputs are finite; a program needn't handle non-finite values.
Results may differ from a plain program's by a relative error of at most 0.015.
Values may be sent and summed in bfloat16 or wider, within the bound.
A program may use at most 128 MiB of HBM per device.

v0:
```python
import jax
import jax.numpy as jnp
from jax import lax
from jax.sharding import PartitionSpec as P


def per_device(lookup_ids, table_feature, tables, cross_down, cross_up, cross_bias):
    slots_local = tables.shape[0]
    feats = table_feature.shape[0]
    sources = lax.axis_size("batch")
    groups = lax.axis_size("mp")
    examples_local = lookup_ids.shape[1] // sources
    share = examples_local // groups
    start = lax.axis_index("mp") * share
    by_owner = lookup_ids.reshape(slots_local, sources, examples_local)
    wanted = lax.dynamic_slice_in_dim(by_owner, start, share, 2)
    looked = jnp.stack(
        [
            jnp.take(tables[slot], wanted[slot].reshape(sources * share), axis=0)
            for slot in range(slots_local)
        ],
        axis=1,
    )
    looked = looked.reshape(sources, share, slots_local, tables.shape[2])
    received = lax.all_to_all(
        lax.all_to_all(looked, "batch", split_axis=0, concat_axis=0, tiled=True),
        "mp",
        split_axis=3,
        concat_axis=1,
        tiled=True,
    )
    emb_local = received.shape[3]
    unfolded = jnp.transpose(received, (1, 0, 2, 3)).reshape(examples_local, feats, emb_local)
    placing = (table_feature[:, None] == jnp.arange(feats, dtype=jnp.int32)[None, :]).astype(
        jnp.bfloat16
    )
    ordered = jnp.einsum("rse,sf->ref", unfolded, placing, preferred_element_type=jnp.float32)
    embedded = ordered.astype(jnp.bfloat16).reshape(examples_local, emb_local * feats)
    embedded_wide = embedded.astype(jnp.float32)
    state = embedded
    for layer in range(len(cross_down)):
        weight_down = cross_down[layer]
        term = jnp.dot(state, weight_down, preferred_element_type=jnp.float32)
        term = term.astype(jnp.bfloat16).astype(jnp.float32)
        low = lax.psum(term.astype(jnp.bfloat16), "mp")
        high = (
            jnp.dot(low, cross_up[layer], preferred_element_type=jnp.float32)
            + cross_bias[layer][None, :]
        )
        state = (embedded_wide * high + state.astype(jnp.float32)).astype(jnp.bfloat16)
    return state


def solution(mesh):
    return jax.shard_map(
        per_device,
        mesh=mesh,
        in_specs=(
            P("batch", None),
            P(),
            P("batch", None, None),
            P(None, "mp", None),
            P(None, None, "mp"),
            P(None, "mp"),
        ),
        out_specs=P("batch", "mp"),
        check_vma=False,
    )
```

profile of v0, /device:TPU:0, one launch (start us, length us, event | category | flops | bytes accessed | tf_op | source)
XLA Modules:
  0.0 718.1 jit_solution(7940920189103681202)
XLA Ops:
  8.9 11.4 %slice_bitcast_fusion = (bf16[8192,128]{1,0:T(8,128)(2,1)}, bf16[8192,128]{1,0:T(8,128)(2,1)}, bf16[8192,128]{1,0:T(8,128)(2,1)}, bf16[8192,128]{1,0:T(8,128)(2,...) fusion(bf16[8,8192,128]{2,1,0:T(8,128)(2,1)} %param.10), kind=kLoop, calls=%fused_computation.27 | loop fusion | bytes 33554432 | tf_op jit(solution)/shard_map/squeeze | solution.py:19
  20.4 12.9 %gather_fusion.1 = bf16[4096,128]{1,0:T(8,128)(2,1)S(1)} fusion(bf16[8192,128]{1,0:T(8,128)(2,1)} %get-tuple-element.11, s32[4096]{0:T(1024)S(1)} %fusion.21), kind=kCustom, calls=%fused_computation.1.clone | custom fusion | bytes 2113536 | tf_op jit(solution)/shard_map/jit(_take)/gather | solution.py:19
  42.1 12.9 %gather_fusion.2 = bf16[4096,128]{1,0:T(8,128)(2,1)S(1)} fusion(bf16[8192,128]{1,0:T(8,128)(2,1)} %get-tuple-element.10, s32[4096]{0:T(1024)S(1)} %fusion.22), kind=kCustom, calls=%fused_computation.2.clone | custom fusion | bytes 2113536 | tf_op jit(solution)/shard_map/jit(_take)/gather | solution.py:19
  63.9 12.9 %gather_fusion.3 = bf16[4096,128]{1,0:T(8,128)(2,1)S(1)} fusion(bf16[8192,128]{1,0:T(8,128)(2,1)} %get-tuple-element.9, s32[4096]{0:T(1024)S(1)} %fusion.23), kind=kCustom, calls=%fused_computation.3.clone | custom fusion | bytes 2113536 | tf_op jit(solution)/shard_map/jit(_take)/gather | solution.py:19
  79.7 6.0 copy.44
  85.7 12.9 %gather_fusion.4 = bf16[4096,128]{1,0:T(8,128)(2,1)S(1)} fusion(bf16[8192,128]{1,0:T(8,128)(2,1)} %get-tuple-element.8, s32[4096]{0:T(1024)S(1)} %fusion.24), kind=kCustom, calls=%fused_computation.4.clone | custom fusion | bytes 2113536 | tf_op jit(solution)/shard_map/jit(_take)/gather | solution.py:19
  107.5 12.9 %gather_fusion.5 = bf16[4096,128]{1,0:T(8,128)(2,1)S(1)} fusion(bf16[8192,128]{1,0:T(8,128)(2,1)} %get-tuple-element.7, s32[4096]{0:T(1024)S(1)} %fusion.25), kind=kCustom, calls=%fused_computation.5.clone | custom fusion | bytes 2113536 | tf_op jit(solution)/shard_map/jit(_take)/gather | solution.py:19
  123.3 6.0 copy.46
  129.3 12.9 %gather_fusion.6 = bf16[4096,128]{1,0:T(8,128)(2,1)S(1)} fusion(bf16[8192,128]{1,0:T(8,128)(2,1)} %get-tuple-element.13, s32[4096]{0:T(1024)S(1)} %fusion.26), kind=kCustom, calls=%fused_computation.6.clone | custom fusion | bytes 2113536 | tf_op jit(solution)/shard_map/jit(_take)/gather | solution.py:19
  151.0 12.9 %gather_fusion.7 = bf16[4096,128]{1,0:T(8,128)(2,1)S(1)} fusion(bf16[8192,128]{1,0:T(8,128)(2,1)} %get-tuple-element.6, s32[4096]{0:T(1024)S(1)} %fusion.27), kind=kCustom, calls=%fused_computation.7.clone | custom fusion | bytes 2113536 | tf_op jit(solution)/shard_map/jit(_take)/gather | solution.py:19
  172.8 12.1 %gather_fusion = bf16[4096,128]{1,0:T(8,128)(2,1)S(1)} fusion(bf16[8192,128]{1,0:T(8,128)(2,1)S(1)} %get-tuple-element.12, s32[4096]{0:T(1024)S(1)} %fusion.20), kind=kCustom, calls=%fused_computation.clone | custom fusion | bytes 2113536 | tf_op jit(solution)/shard_map/jit(_take)/gather | solution.py:19
  193.8 42.8 %stack.35 = bf16[8,512,8,128]{1,2,3,0:T(8,128)(2,1)} concatenate(bf16[8,512,1,128]{1,2,3,0:T(2,128)(2,1)} %copy.41, bf16[8,512,1,128]{1,2,3,0:T(2,128)(2,1)S(1)} %copy-done.1, bf16[8,512,1,128]{1,2,3,0:T(2,128)(2,1)} %copy.43, bf16[8,512,1,128]{1,2,3,0:T(2,128)(2,1)} %copy.44, bf16[8,512,1,128]{1,2,3,0:T(2,128)(2,1)} %copy.45, bf16[8,512,1,128]{1,2,3,0:T(2,128)(2,1)} %copy.46, ...), dimensions={2} | concatenate | bytes 16777216 | tf_op jit(solution)/shard_map/stack | solution.py:17
  236.5 190.6 %all_to_all.23 = bf16[8,512,8,128]{1,2,3,0:T(8,128)(2,1)} all-to-all(bf16[8,512,8,128]{1,2,3,0:T(8,128)(2,1)} %stack.35), channel_id=1, replica_groups=mesh['batch'=8,'mp'=4] {'batch'}, dimensions={0} | all-to-all | bytes 16777216 | tf_op jit(solution)/shard_map/all_to_all | solution.py:26
  427.2 8.1 %copy.49 = bf16[8,512,8,128]{1,2,0,3:T(8,128)(2,1)} copy(bf16[8,512,8,128]{1,2,3,0:T(8,128)(2,1)} %all_to_all.23) | data formatting | bytes 16777216 | tf_op jit(solution)/shard_map/all_to_all | solution.py:26
  435.2 97.2 %all_to_all.24 = bf16[8,512,8,128]{1,2,0,3:T(8,128)(2,1)S(1)} all-to-all(bf16[8,512,8,128]{1,2,0,3:T(8,128)(2,1)} %copy.49), channel_id=1, replica_groups=mesh['batch'=8,'mp'=4] {'mp'}, dimensions={3} | all-to-all | bytes 16777216 | tf_op jit(solution)/shard_map/all_to_all | solution.py:25
  532.4 7.3 %copy.51 = bf16[8,4,512,8,32]{2,1,4,3,0:T(4,128)(2,1)} copy(bf16[8,4,512,8,32]{2,3,0,4,1:T(8,128)(2,1)S(1)} %bitcast.69) | data formatting | bytes 16777216 | tf_op jit(solution)/shard_map/all_to_all | solution.py:25
  539.7 14.4 %all_to_all.20 = bf16[8,2048,8,32]{1,3,2,0:T(8,128)(2,1)} reshape(bf16[8,4,512,8,32]{2,1,4,3,0:T(4,128)(2,1)} %copy.51) | data formatting | bytes 16777216 | tf_op jit(solution)/shard_map/all_to_all | solution.py:25
  554.1 10.1 %fusion.6 = bf16[2048,32,64]{0,2,1:T(8,128)(2,1)S(1)} fusion(bf16[2048,8,8,32]{0,3,2,1:T(8,128)(2,1)} %bitcast.68, s32[64]{0:T(128)S(1)} %copy-done.3), kind=kOutput, calls=%fused_computation.16 | convolution fusion | flops 541069312 | bytes 16777472 | tf_op jit(solution)/shard_map/rse,sf->ref/dot_general | solution.py:37
  567.6 7.3 %convolution_convert_fusion.1 = bf16[2048,512]{1,0:T(8,128)(2,1)} fusion(bf16[2048,2048]{0,1:T(8,128)(2,1)S(1)} %bitcast.66, bf16[2,2048,512]{2,1,0:T(8,128)(2,1)} %param.11), kind=kOutput, calls=%fused_computation.18 | convolution fusion | flops 4296015872 | bytes 12582912 | tf_op jit(solution)/shard_map/dot_general | solution.py:43
  575.0 11.9 %copy.53 = bf16[2048,2048]{1,0:T(8,128)(2,1)} copy(bf16[2048,2048]{0,1:T(8,128)(2,1)} %bitcast.67) | data formatting | bytes 16777216 | tf_op jit(solution)/shard_map/reshape | solution.py:38
  586.9 37.5 %all-reduce.3.cloned.1.call-done = bf16[2048,512]{1,0:T(8,128)(2,1)} async-done(((bf16[2048,512]{1,0:T(8,128)(2,1)}), bf16[2048,512]{1,0:T(8,128)(2,1)}) %all-reduce.3.cloned.1.call-update) | async-done | bytes 2097168 | tf_op jit(solution)/shard_map/psum | solution.py:45
  624.4 9.9 %fusion.2 = bf16[2048,2048]{1,0:T(8,128)(2,1)S(1)} fusion(bf16[2048,2048]{1,0:T(8,128)(2,1)} %copy.53, f32[2048]{0:T(1024)S(1)} %bitcast.96, bf16[2048,512]{1,0:T(8,128)(2,1)} %all-reduce.3.cloned.1.call-done, bf16[2,512,2048]{2,1,0:T(8,128)(2,1)} %param.12), kind=kOutput, calls=%fused_computation.12 | convolution fusion | flops 4315938816 | bytes 20979712 | tf_op jit(solution)/shard_map/dot_general | solution.py:47
  643.8 51.6 %all-reduce.5.cloned.1.call-done = bf16[2048,512]{1,0:T(8,128)(2,1)} async-done(((bf16[2048,512]{1,0:T(8,128)(2,1)}), bf16[2048,512]{1,0:T(8,128)(2,1)}) %all-reduce.5.cloned.1.call-update) | async-done | bytes 2097168 | tf_op jit(solution)/shard_map/psum | solution.py:45
  695.4 15.9 %fusion.1 = bf16[2048,2048]{1,0:T(8,128)(2,1)} fusion(bf16[2048,2048]{1,0:T(8,128)(2,1)} %copy.53, bf16[2048,2048]{1,0:T(8,128)(2,1)} %copy-done.5, f32[2048]{0:T(1024)S(1)} %bitcast.95, bf16[2048,512]{1,0:T(8,128)(2,1)} %all-reduce.5.cloned.1.call-done, bf16[2,512,2048]{2,1,0:T(8,128)(2,1)} %param.12), kind=kOutput, calls=%fused_computation.11 | convolution fusion | flops 4320133120 | bytes 29368320 | tf_op jit(solution)/shard_map/dot_general | solution.py:47
  (49 shorter events, 74.0 us)
Async XLA Ops:
  6.5 617.9 %all-reduce.3.cloned.1.call-start = ((), (), s32[]{:S(2)}) async-start(), calls=%async_computation.2 | async-start | bytes 4194304 | tf_op jit(solution)/shard_map/psum | solution.py:45
  184.9 8.8 %copy-start.1 = (bf16[8,512,1,128]{1,2,3,0:T(2,128)(2,1)S(1)}, bf16[8,512,1,128]{1,2,3,0:T(2,128)(2,1)}, u32[]{:S(2)}) copy-start(bf16[8,512,1,128]{1,2,3,0:T(2,128)(2,1)} %copy.42) | copy-start | bytes 3145732
  539.7 14.4 %copy-start.3 = (s32[64]{0:T(128)S(1)}, s32[64]{0:T(128)}, u32[]{:S(2)}) copy-start(s32[64]{0:T(128)} %param.9) | copy-start | bytes 772
  564.2 3.4 copy-start
  567.6 7.4 %copy-start.2 = (f32[2,2048]{1,0:T(2,128)S(1)}, f32[2,2048]{1,0:T(2,128)}, u32[]{:S(2)}) copy-start(f32[2,2048]{1,0:T(2,128)} %param.13) | copy-start | bytes 49156
  575.0 120.4 %all-reduce.5.cloned.1.call-start = ((), (), s32[]{:S(2)}) async-start(), calls=%async_computation.3 | async-start | bytes 4194304 | tf_op jit(solution)/shard_map/psum | solution.py:45
  624.4 13.3 %copy-start.4 = (bf16[2,2048,512]{2,1,0:T(8,128)(2,1)S(1)}, bf16[2,2048,512]{2,1,0:T(8,128)(2,1)}, u32[]{:S(2)}) copy-start(bf16[2,2048,512]{2,1,0:T(8,128)(2,1)} %param.11) | copy-start | bytes 12582916
  634.4 3.4 copy-start.5
Sparse Core Ops, SparseCore 0:
  575.1 49.3 all-reduce.2
  643.9 51.4 all-reduce.4
where the time goes:
time: 725 us; the launch traced here: 718 us
  blocking collectives  288 us (40%)
  local copies, waits for them, and re-layouts  255 us (35%)
  waiting for transfers between devices  89.2 us (12%)
  matrix products  49.2 us (7%)
  other arithmetic  23.4 us (3%)
  between operations  13.7 us (2%)
    all_to_all x1, blocking collectives, per_device(): lax.all_to_all(looked, 'batch', split_axis=0, concat_axis=0, tiled=True)  191 us
    gather x8, local copies, waits for them, and re-layouts, per_device(): jnp.take(tables[slot], wanted[slot].reshape(sources * share), axis=0)  102 us
    all_to_all x1, blocking collectives, per_device(): lax.all_to_all(lax.all_to_all(looked, 'batch', split_axis=0, concat_axis=...  97.2 us
    another operation x9, local copies, waits for them, and re-layouts, per_device(): jnp.stack([jnp.take(tables[slot], wanted[slot].reshape(sources * share),...  90.5 us
    psum x2, waiting for transfers between devices, per_device(): low = lax.psum(term.astype(jnp.bfloat16), 'mp')  89.1 us
    dot_general x2, matrix products, per_device(): jnp.dot(low, cross_up[layer], preferred_element_type=jnp.float32)  25.8 us
    select_n x8, other arithmetic, per_device(): jnp.take(tables[slot], wanted[slot].reshape(sources * share), axis=0)  23.3 us
    all_to_all x2, local copies, waits for them, and re-layouts, per_device(): lax.all_to_all(lax.all_to_all(looked, 'batch', split_axis=0, concat_axis=...  21.7 us
  transfers between devices with their start and end apart: 2, of which 2 were waited for; matrix products, arithmetic and copies ran while one was open for 2% of the time, Pallas kernels for 0%

commit v1 on v0

--- a/solution.py
+++ b/solution.py
@@ -22,13 +22,14 @@
         axis=1,
     )
     looked = looked.reshape(sources, share, slots_local, tables.shape[2])
-    received = lax.all_to_all(
-        lax.all_to_all(looked, "batch", split_axis=0, concat_axis=0, tiled=True),
-        "mp",
-        split_axis=3,
-        concat_axis=1,
-        tiled=True,
-    )
+
+    def note_lanes(array_here):
+        mixed_arr = lax.all_to_all(
+            jnp.stack(jnp.split(array_here, lax.axis_size("mp"), 3), axis=0), "mp", 0, 0
+        )
+        return jnp.concatenate(mixed_arr, 1)
+
+    received = note_lanes(lax.all_to_all(looked, "batch", split_axis=0, concat_axis=0, tiled=True))
     emb_local = received.shape[3]
     unfolded = jnp.transpose(received, (1, 0, 2, 3)).reshape(examples_local, feats, emb_local)
     placing = (table_feature[:, None] == jnp.arange(feats, dtype=jnp.int32)[None, :]).astype(

time: 725 us -> 667 us (0.920)
  local copies, waits for them, and re-layouts: 255 us -> 196 us
    another operation x9 -> x1, local copies, waits for them, and re-layouts: 90.5 us -> 1.15 us  [per_device(): jnp.stack([jnp.take(tables[slot], wanted[slot].reshape(sources * share),...]
    another operation x0 -> x5, local copies, waits for them, and re-layouts: none -> 43.8 us  [note_lanes(): jnp.stack(jnp.split(array_here, lax.axis_size('mp'), 3), axis=0)]
    all_to_all x3 -> x0, local copies, waits for them, and re-layouts: 29.7 us -> none  [the longest x2 21.7 us: per_device(): lax.all_to_all(lax.all_to_all(looked, 'batch', split_axis=0, concat_axis=...]
    reshape x0 -> x1, local copies, waits for them, and re-layouts: none -> 8.12 us  [note_lanes(): return jnp.concatenate(mixed_arr, 1)]
    unnamed x12 -> x17, local copies, waits for them, and re-layouts: 6.8 us -> 14.9 us
where the time goes in v1:
time: 667 us; the launch traced here: 657 us
  blocking collectives  288 us (43%)
  local copies, waits for them, and re-layouts  196 us (29%)
  waiting for transfers between devices  89.4 us (13%)
  matrix products  49.4 us (7%)
  other arithmetic  21.1 us (3%)
  between operations  13.9 us (2%)
    all_to_all x1, blocking collectives, per_device(): lax.all_to_all(looked, 'batch', split_axis=0, concat_axis=0, tiled=True)  191 us
    gather x8, local copies, waits for them, and re-layouts, per_device(): jnp.take(tables[slot], wanted[slot].reshape(sources * share), axis=0)  102 us
    all_to_all x1, blocking collectives, note_lanes(): lax.all_to_all(jnp.stack(jnp.split(array_here, lax.axis_size('mp'), 3), a...  96.8 us
    psum x2, waiting for transfers between devices, per_device(): low = lax.psum(term.astype(jnp.bfloat16), 'mp')  89.3 us
    another operation x5, local copies, waits for them, and re-layouts, note_lanes(): jnp.stack(jnp.split(array_here, lax.axis_size('mp'), 3), axis=0)  43.8 us
    dot_general x2, matrix products, per_device(): jnp.dot(low, cross_up[layer], preferred_element_type=jnp.float32)  25.8 us
    select_n x8, other arithmetic, per_device(): jnp.take(tables[slot], wanted[slot].reshape(sources * share), axis=0)  17.2 us
    unnamed x17, local copies, waits for them, and re-layouts  14.9 us
  transfers between devices with their start and end apart: 2, of which 2 were waited for; matrix products, arithmetic and copies ran while one was open for 2% of the time, Pallas kernels for 0%

profile of v1, /device:TPU:0, one launch (start us, length us, event | category | flops | bytes accessed | tf_op | source)
XLA Modules:
  0.0 657.3 jit_solution(1250544411446974405)
XLA Ops:
  8.9 11.5 %slice_bitcast_fusion.4 = (bf16[8192,128]{1,0:T(8,128)(2,1)S(1)}, bf16[8192,128]{1,0:T(8,128)(2,1)}, bf16[8192,128]{1,0:T(8,128)(2,1)}, bf16[8192,128]{1,0:T(8,1...) fusion(bf16[8,8192,128]{2,1,0:T(8,128)(2,1)} %param.10), kind=kLoop, calls=%fused_computation.32 | loop fusion | bytes 33554432 | tf_op jit(solution)/shard_map/squeeze | solution.py:19
  20.3 12.9 %gather_fusion = bf16[4096,128]{1,0:T(8,128)(2,1)S(1)} fusion(bf16[8192,128]{1,0:T(8,128)(2,1)} %get-tuple-element.12, s32[4096]{0:T(1024)S(1)} %get-tuple-element.28), kind=kCustom, calls=%fused_computation.clone | custom fusion | bytes 2113536 | tf_op jit(solution)/shard_map/jit(_take)/gather | solution.py:19
  36.5 12.9 %gather_fusion.1 = bf16[4096,128]{1,0:T(8,128)(2,1)S(1)} fusion(bf16[8192,128]{1,0:T(8,128)(2,1)} %get-tuple-element.11, s32[4096]{0:T(1024)S(1)} %get-tuple-element.29), kind=kCustom, calls=%fused_computation.1.clone | custom fusion | bytes 2113536 | tf_op jit(solution)/shard_map/jit(_take)/gather | solution.py:19
  52.7 12.9 %gather_fusion.2 = bf16[4096,128]{1,0:T(8,128)(2,1)S(1)} fusion(bf16[8192,128]{1,0:T(8,128)(2,1)} %get-tuple-element.10, s32[4096]{0:T(1024)S(1)} %get-tuple-element.30), kind=kCustom, calls=%fused_computation.2.clone | custom fusion | bytes 2113536 | tf_op jit(solution)/shard_map/jit(_take)/gather | solution.py:19
  69.0 12.9 %gather_fusion.3 = bf16[4096,128]{1,0:T(8,128)(2,1)S(1)} fusion(bf16[8192,128]{1,0:T(8,128)(2,1)} %get-tuple-element.9, s32[4096]{0:T(1024)S(1)} %get-tuple-element.31), kind=kCustom, calls=%fused_computation.3.clone | custom fusion | bytes 2113536 | tf_op jit(solution)/shard_map/jit(_take)/gather | solution.py:19
  85.2 12.9 %gather_fusion.4 = bf16[4096,128]{1,0:T(8,128)(2,1)S(1)} fusion(bf16[8192,128]{1,0:T(8,128)(2,1)} %get-tuple-element.8, s32[4096]{0:T(1024)S(1)} %get-tuple-element.32), kind=kCustom, calls=%fused_computation.4.clone | custom fusion | bytes 2113536 | tf_op jit(solution)/shard_map/jit(_take)/gather | solution.py:19
  101.4 12.9 %gather_fusion.5 = bf16[4096,128]{1,0:T(8,128)(2,1)S(1)} fusion(bf16[8192,128]{1,0:T(8,128)(2,1)} %get-tuple-element.7, s32[4096]{0:T(1024)S(1)} %get-tuple-element.33), kind=kCustom, calls=%fused_computation.5.clone | custom fusion | bytes 2113536 | tf_op jit(solution)/shard_map/jit(_take)/gather | solution.py:19
  117.6 12.9 %gather_fusion.6 = bf16[4096,128]{1,0:T(8,128)(2,1)S(1)} fusion(bf16[8192,128]{1,0:T(8,128)(2,1)} %get-tuple-element.13, s32[4096]{0:T(1024)S(1)} %get-tuple-element.34), kind=kCustom, calls=%fused_computation.6.clone | custom fusion | bytes 2113536 | tf_op jit(solution)/shard_map/jit(_take)/gather | solution.py:19
  133.8 12.1 %gather_fusion.7 = bf16[4096,128]{1,0:T(8,128)(2,1)S(1)} fusion(bf16[8192,128]{1,0:T(8,128)(2,1)S(1)} %get-tuple-element.6, s32[4096]{0:T(1024)S(1)} %get-tuple-element.35), kind=kCustom, calls=%fused_computation.7.clone | custom fusion | bytes 2113536 | tf_op jit(solution)/shard_map/jit(_take)/gather | solution.py:19
  149.2 190.8 %all_to_all.10 = bf16[8,512,8,128]{3,1,2,0:T(8,128)(2,1)S(1)} all-to-all(bf16[8,512,8,128]{3,1,2,0:T(8,128)(2,1)} %constant_dynamic-update-slice_fusion), channel_id=1, replica_groups=mesh['batch'=8,'mp'=4] {'batch'}, dimensions={0} | all-to-all | bytes 16777216 | tf_op jit(solution)/shard_map/all_to_all | solution.py:32
  340.1 13.0 %slice_bitcast_fusion.3 = (bf16[1,8,512,8,32]{4,2,3,1,0:T(8,128)(2,1)}, bf16[1,8,512,8,32]{4,2,3,1,0:T(8,128)(2,1)}, bf16[1,8,512,8,32]{4,2,3,1,0:T(8,128)(2,1)}, bf16[1,8,512,8,32]{4,2,3,1,0:T(8,128)(2,1)}) fusion(bf16[8,512,8,128]{3,1,2,0:T(8,128)(2,1)S(1)} %all_to_all.10), kind=kLoop, calls=%fused_computation.16 | loop fusion | bytes 16777216 | tf_op jit(solution)/shard_map/stack | solution.py:28
  353.1 6.7 %copy.30 = bf16[1,8,512,8,32]{2,4,3,1,0:T(8,128)(2,1)S(1)} copy(bf16[1,8,512,8,32]{4,2,3,1,0:T(8,128)(2,1)} %get-tuple-element.14) | data formatting | bytes 4194304 | tf_op jit(solution)/shard_map/stack | solution.py:28
  359.8 8.1 %copy.31 = bf16[1,8,512,8,32]{2,4,3,1,0:T(8,128)(2,1)} copy(bf16[1,8,512,8,32]{4,2,3,1,0:T(8,128)(2,1)} %get-tuple-element.17) | data formatting | bytes 4194304 | tf_op jit(solution)/shard_map/stack | solution.py:28
  367.8 8.0 %copy.32 = bf16[1,8,512,8,32]{2,4,3,1,0:T(8,128)(2,1)} copy(bf16[1,8,512,8,32]{4,2,3,1,0:T(8,128)(2,1)} %get-tuple-element.16) | data formatting | bytes 4194304 | tf_op jit(solution)/shard_map/stack | solution.py:28
  375.9 8.0 %copy.33 = bf16[1,8,512,8,32]{2,4,3,1,0:T(8,128)(2,1)} copy(bf16[1,8,512,8,32]{4,2,3,1,0:T(8,128)(2,1)} %get-tuple-element.15) | data formatting | bytes 4194304 | tf_op jit(solution)/shard_map/stack | solution.py:28
  387.7 96.8 %all_to_all.11 = bf16[4,8,512,8,32]{2,4,3,1,0:T(8,128)(2,1)} all-to-all(bf16[4,8,512,8,32]{2,4,3,1,0:T(8,128)(2,1)S(1)} %pad_maximum_fusion), channel_id=1, replica_groups=mesh['batch'=8,'mp'=4] {'mp'}, dimensions={0} | all-to-all | bytes 16777216 | tf_op jit(solution)/shard_map/all_to_all | solution.py:27
  484.6 8.1 %copy.37 = bf16[4,8,8,4,8,512]{5,4,0,3,2,1:T(8,128)(2,1)} copy(bf16[4,8,8,4,8,512]{5,4,3,2,1,0:T(8,128)(2,1)} %bitcast.92) | data formatting | bytes 16777216 | tf_op jit(solution)/shard_map/reshape | solution.py:30
  492.7 10.1 %fusion.6 = bf16[2048,32,64]{0,2,1:T(8,128)(2,1)S(1)} fusion(bf16[2048,8,8,32]{0,3,2,1:T(8,128)(2,1)} %bitcast.91, s32[64]{0:T(128)S(1)} %copy-done.2), kind=kOutput, calls=%fused_computation.21 | convolution fusion | flops 541069312 | bytes 16777472 | tf_op jit(solution)/shard_map/rse,sf->ref/dot_general | solution.py:38
  506.2 7.4 %convolution_convert_fusion.1 = bf16[2048,512]{1,0:T(8,128)(2,1)} fusion(bf16[2048,2048]{0,1:T(8,128)(2,1)S(1)} %bitcast.89, bf16[2,2048,512]{2,1,0:T(8,128)(2,1)} %param.11), kind=kOutput, calls=%fused_computation.23 | convolution fusion | flops 4296015872 | bytes 12582912 | tf_op jit(solution)/shard_map/dot_general | solution.py:44
  513.8 11.7 %copy.36 = bf16[2048,2048]{1,0:T(8,128)(2,1)} copy(bf16[2048,2048]{0,1:T(8,128)(2,1)} %bitcast.90) | data formatting | bytes 16777216 | tf_op jit(solution)/shard_map/reshape | solution.py:39
  525.5 37.7 %all-reduce.3.cloned.1.call-done = bf16[2048,512]{1,0:T(8,128)(2,1)} async-done(((bf16[2048,512]{1,0:T(8,128)(2,1)}), bf16[2048,512]{1,0:T(8,128)(2,1)}) %all-reduce.3.cloned.1.call-update) | async-done | bytes 2097168 | tf_op jit(solution)/shard_map/psum | solution.py:46
  563.2 10.0 %fusion.2 = bf16[2048,2048]{1,0:T(8,128)(2,1)S(1)} fusion(bf16[2048,2048]{1,0:T(8,128)(2,1)} %copy.36, f32[2048]{0:T(1024)S(1)} %bitcast.119, bf16[2048,512]{1,0:T(8,128)(2,1)} %all-reduce.3.cloned.1.call-done, bf16[2,512,2048]{2,1,0:T(8,128)(2,1)} %param.12), kind=kOutput, calls=%fused_computation.12 | convolution fusion | flops 4315938816 | bytes 20979712 | tf_op jit(solution)/shard_map/dot_general | solution.py:48
  582.7 51.6 %all-reduce.5.cloned.1.call-done = bf16[2048,512]{1,0:T(8,128)(2,1)} async-done(((bf16[2048,512]{1,0:T(8,128)(2,1)}), bf16[2048,512]{1,0:T(8,128)(2,1)}) %all-reduce.5.cloned.1.call-update) | async-done | bytes 2097168 | tf_op jit(solution)/shard_map/psum | solution.py:46
  634.4 15.9 %fusion.1 = bf16[2048,2048]{1,0:T(8,128)(2,1)} fusion(bf16[2048,2048]{1,0:T(8,128)(2,1)} %copy.36, bf16[2048,2048]{1,0:T(8,128)(2,1)} %copy-done.4, f32[2048]{0:T(1024)S(1)} %bitcast.118, bf16[2048,512]{1,0:T(8,128)(2,1)} %all-reduce.5.cloned.1.call-done, bf16[2,512,2048]{2,1,0:T(8,128)(2,1)} %param.12), kind=kOutput, calls=%fused_computation.11 | convolution fusion | flops 4320133120 | bytes 29368320 | tf_op jit(solution)/shard_map/dot_general | solution.py:48
  (46 shorter events, 45.7 us)
Async XLA Ops:
  6.5 556.7 %all-reduce.3.cloned.1.call-start = ((), (), s32[]{:S(2)}) async-start(), calls=%async_computation.2 | async-start | bytes 4194304 | tf_op jit(solution)/shard_map/psum | solution.py:46
  484.6 8.1 %copy-start.2 = (s32[64]{0:T(128)S(1)}, s32[64]{0:T(128)}, u32[]{:S(2)}) copy-start(s32[64]{0:T(128)} %param.9) | copy-start | bytes 772
  502.8 3.4 copy-start
  506.2 7.6 %copy-start.1 = (f32[2,2048]{1,0:T(2,128)S(1)}, f32[2,2048]{1,0:T(2,128)}, u32[]{:S(2)}) copy-start(f32[2,2048]{1,0:T(2,128)} %param.13) | copy-start | bytes 49156
  513.6 120.8 %all-reduce.5.cloned.1.call-start = ((), (), s32[]{:S(2)}) async-start(), calls=%async_computation.3 | async-start | bytes 4194304 | tf_op jit(solution)/shard_map/psum | solution.py:46
  563.2 13.4 %copy-start.3 = (bf16[2,2048,512]{2,1,0:T(8,128)(2,1)S(1)}, bf16[2,2048,512]{2,1,0:T(8,128)(2,1)}, u32[]{:S(2)}) copy-start(bf16[2,2048,512]{2,1,0:T(8,128)(2,1)} %param.11) | copy-start | bytes 12582916
  573.2 3.4 copy-start.4
Sparse Core Ops, SparseCore 0:
  513.7 49.4 all-reduce.2
  582.9 51.4 all-reduce.4
